TPU v7x, 64 devices: a 2x2x8 block of a 4x4x8 slice. The times are simulated.
64 devices in a mesh: dp: 4 (over x, y), cp: 16 (over z, core).
Axes of the slice: x: 2, y: 2, z: 8, core: 2. Of those that a mesh axis runs over, the one named last changes fastest.
The devices are a block of a 4x4x8 slice.
Arguments:
- x_in: bfloat16 [8192, 3584], P(('dp', 'cp')), parts along dimension 0
- dy_in: bfloat16 [8192, 3584], P(('dp', 'cp')), parts along dimension 0
- w_q: bfloat16 [3584, 3584], replicated
- w_k: bfloat16 [3584, 512], replicated
- w_v: bfloat16 [3584, 512], replicated
- w_o: bfloat16 [3584, 3584], replicated
Outputs:
- output 1: bfloat16 [8192, 3584], P(('dp', 'cp')), parts along dimension 0
- output 2: bfloat16 [8192, 3584], P(('dp', 'cp')), parts along dimension 0
There are 4 independent parts. A program takes and returns all parts, laid end to end along the dimension named above; an argument that names none is the same for every part.
All inputs are finite; a program needn't handle non-finite values.
Results may differ from a plain program's by a relative error of at most 0.0109693.
Values are sent between devices in bfloat16 or wider.
A program may use at most 768 MiB of HBM per device.

v0:
```python
import jax
import jax.numpy as jnp
from jax import lax
from jax.sharding import PartitionSpec as P

HEAD_DIM = 128
SCORE_LIMIT = 8388608


def block_rows(n_rows, n_heads, n_keys):
    blk_rows = n_rows
    for step_idx in range(30):
        if blk_rows % 2 == 0 and blk_rows > 8 and blk_rows * n_heads * n_keys > SCORE_LIMIT:
            blk_rows = blk_rows // 2
    return blk_rows


def split_rows(array_in, blk_rows):
    return array_in.reshape((array_in.shape[0] // blk_rows, blk_rows) + array_in.shape[1:])


def project(rows_in, weight):
    return jnp.dot(rows_in, weight, preferred_element_type=jnp.float32).astype(jnp.bfloat16)


def attend_forward(q_loc, k_all, v_all, blk_rows):
    n_rows, kv_heads, q_group, head_dim = q_loc.shape
    score_scale = head_dim ** -0.5

    def one_block(q_blk):
        scores = jnp.einsum("thjd,uhd->thju", q_blk, k_all, preferred_element_type=jnp.float32) * score_scale
        lse_blk = jax.nn.logsumexp(scores, axis=-1, keepdims=True)
        prob_bf = jnp.exp(scores - lse_blk).astype(jnp.bfloat16)
        out_blk = jnp.einsum("thju,uhd->thjd", prob_bf, v_all, preferred_element_type=jnp.float32).astype(jnp.bfloat16)
        return out_blk, lse_blk

    out_blocks, lse_blocks = lax.map(one_block, split_rows(q_loc, blk_rows))
    return out_blocks.reshape(n_rows, kv_heads, q_group, head_dim), lse_blocks.reshape(n_rows, kv_heads, q_group, 1)


def attend_backward(q_loc, k_all, v_all, lse_loc, delta_loc, do_loc, blk_rows):
    n_rows, kv_heads, q_group, head_dim = q_loc.shape
    score_scale = head_dim ** -0.5

    def one_block(acc_pair, block_in):
        dk_acc, dv_acc = acc_pair
        q_blk, do_blk, lse_blk, delta_blk = block_in
        scores = jnp.einsum("thjd,uhd->thju", q_blk, k_all, preferred_element_type=jnp.float32) * score_scale
        prob_bf = jnp.exp(scores - lse_blk).astype(jnp.bfloat16)
        dprob = jnp.einsum("thjd,uhd->thju", do_blk, v_all, preferred_element_type=jnp.float32)
        dscore = (prob_bf.astype(jnp.float32) * (dprob - delta_blk)).astype(jnp.bfloat16)
        dq_blk = (jnp.einsum("thju,uhd->thjd", dscore, k_all, preferred_element_type=jnp.float32) * score_scale).astype(jnp.bfloat16)
        dk_acc = dk_acc + jnp.einsum("thju,thjd->uhd", dscore, q_blk, preferred_element_type=jnp.float32) * score_scale
        dv_acc = dv_acc + jnp.einsum("thju,thjd->uhd", prob_bf, do_blk, preferred_element_type=jnp.float32)
        return (dk_acc, dv_acc), dq_blk

    zero_acc = jnp.zeros(k_all.shape, jnp.float32)
    blocks_in = (split_rows(q_loc, blk_rows), split_rows(do_loc, blk_rows), split_rows(lse_loc, blk_rows), split_rows(delta_loc, blk_rows))
    acc_final, dq_blocks = lax.scan(one_block, (zero_acc, zero_acc), blocks_in)
    return dq_blocks.reshape(n_rows, kv_heads * q_group * head_dim), acc_final[0], acc_final[1]


def solution(mesh):
    n_group = mesh.shape["cp"]
    row_spec = P(("dp", "cp"), None)
    full_spec = P(None, None)

    def local_body(x_loc, dy_loc, w_q, w_k, w_v, w_o):
        n_rows = x_loc.shape[0]
        q_heads = w_q.shape[1] // HEAD_DIM
        kv_heads = w_k.shape[1] // HEAD_DIM
        q_group = q_heads // kv_heads
        blk_rows = block_rows(n_rows, q_heads, n_rows * n_group)
        q_loc = project(x_loc, w_q).reshape(n_rows, kv_heads, q_group, HEAD_DIM)
        k_loc = project(x_loc, w_k).reshape(n_rows, kv_heads, HEAD_DIM)
        v_loc = project(x_loc, w_v).reshape(n_rows, kv_heads, HEAD_DIM)
        k_all = lax.all_gather(k_loc, "cp", axis=0, tiled=True)
        v_all = lax.all_gather(v_loc, "cp", axis=0, tiled=True)
        out_loc, lse_loc = attend_forward(q_loc, k_all, v_all, blk_rows)
        y_loc = project(out_loc.reshape(n_rows, q_heads * HEAD_DIM), w_o)
        do_loc = jnp.einsum("te,ce->tc", dy_loc, w_o, preferred_element_type=jnp.float32).astype(jnp.bfloat16).reshape(n_rows, kv_heads, q_group, HEAD_DIM)
        delta_loc = jnp.einsum("thjd,thjd->thj", do_loc, out_loc, preferred_element_type=jnp.float32)[..., None]
        dq_flat, dk_part, dv_part = attend_backward(q_loc, k_all, v_all, lse_loc, delta_loc, do_loc, blk_rows)
        dk_own = lax.psum_scatter(dk_part, "cp", scatter_dimension=0, tiled=True).astype(jnp.bfloat16).reshape(n_rows, kv_heads * HEAD_DIM)
        dv_own = lax.psum_scatter(dv_part, "cp", scatter_dimension=0, tiled=True).astype(jnp.bfloat16).reshape(n_rows, kv_heads * HEAD_DIM)
        dx_acc = (jnp.einsum("tc,ec->te", dq_flat, w_q, preferred_element_type=jnp.float32)
                  + jnp.einsum("tc,ec->te", dk_own, w_k, preferred_element_type=jnp.float32)
                  + jnp.einsum("tc,ec->te", dv_own, w_v, preferred_element_type=jnp.float32))
        return y_loc, dx_acc.astype(jnp.bfloat16)

    return jax.shard_map(local_body, mesh=mesh,
                         in_specs=(row_spec, row_spec, full_spec, full_spec, full_spec, full_spec),
                         out_specs=(row_spec, row_spec), check_vma=False)
```

profile of v0, /device:TPU:21, one launch (start us, length us, event | category | flops | bytes accessed | tf_op | source)
XLA Modules:
  0.0 254.6 jit_solution(10248434302064439527)
XLA Ops:
  7.3 1.1 copy-done
  8.4 2.7 %fusion.21 = bf16[16,4,8,128]{3,2,1,0:T(8,128)(2,1)S(1)} fusion(bf16[128,3584]{1,0:T(8,128)(2,1)S(1)} %copy-done, bf16[3584,512]{1,0:T(8,128)(2,1)} %param.9), kind=kOutput, calls=%fused_computation.32 | convolution fusion | flops 469827584 | bytes 4718592 | tf_op jit(solution)/shard_map/dot_general | solution.py:23
  11.9 2.7 %convolution_convert_fusion.4 = bf16[128,512]{1,0:T(8,128)(2,1)S(1)} fusion(bf16[128,3584]{1,0:T(8,128)(2,1)S(1)} %copy-done, bf16[3584,512]{1,0:T(8,128)(2,1)} %param.10), kind=kOutput, calls=%fused_computation.31 | convolution fusion | flops 469827584 | bytes 4718592 | tf_op jit(solution)/shard_map/dot_general | solution.py:23
  15.5 11.8 %convolution_convert_fusion.2 = bf16[128,3584]{1,0:T(8,128)(2,1)S(1)} fusion(bf16[128,3584]{1,0:T(8,128)(2,1)S(1)} %copy-done, bf16[3584,3584]{1,0:T(8,128)(2,1)} %param.8), kind=kOutput, calls=%fused_computation.15 | convolution fusion | flops 3288793088 | bytes 27525120 | tf_op jit(solution)/shard_map/dot_general | solution.py:23
  28.1 13.1 %convolution_convert_fusion = bf16[128,3584]{1,0:T(8,128)(2,1)S(1)} fusion(bf16[128,3584]{1,0:T(8,128)(2,1)} %param.7, bf16[3584,3584]{1,0:T(8,128)(2,1)} %param.11), kind=kOutput, calls=%fused_computation.13 | convolution fusion | flops 3288793088 | bytes 27525120 | tf_op jit(solution)/shard_map/te,ce->tc/dot_general | solution.py:81
  41.8 11.4 %all-gather.5.cloned.1.call-done = bf16[2048,4,128]{2,0,1:T(8,128)(2,1)} async-done(((bf16[128,4,128]{2,0,1:T(8,128)(2,1)}), bf16[2048,4,128]{2,0,1:T(8,128)(2,1)}) %all-gather.5.cloned.1.call-update) | async-done | bytes 2097168 | tf_op jit(solution)/shard_map/all_gather | solution.py:77
  53.2 15.2 %bitcast_reduce_fusion = (f32[128,4,7]{0,2,1:T(8,128)S(1)}, f32[4,2048,128,7]{2,1,3,0:T(8,128)}) fusion(bf16[128,4,7,128]{0,3,2,1:T(8,128)(2,1)S(1)} %bitcast.103, bf16[2048,4,128]{2,0,1:T(8,128)(2,1)} %all-gather.5.cloned.1.call-done), kind=kOutput, calls=%fused_computation.5 | convolution fusion | flops 1893724672 | bytes 32389120 | tf_op jit(solution)/shard_map/while/body/eval_jaxpr/thjd,uhd->thju/dot_general | solution.py:31
  68.5 12.7 %fusion.3 = f32[128,4,7]{0,2,1:T(8,128)S(1)} fusion(f32[4,2048,128,7]{2,1,3,0:T(8,128)} %get-tuple-element.31, f32[128,4,7]{0,2,1:T(8,128)S(1)} %is-finite_select_fusion), kind=kLoop, calls=%fused_computation.7 | loop fusion | flops 22016512 | bytes 29388800 | tf_op jit(solution)/shard_map/while/body/eval_jaxpr/reduce_sum | solution.py:32
  81.2 5.0 %copy-done.2 = f32[4,2048,128,7]{2,1,3,0:T(8,128)S(1)} copy-done((f32[4,2048,128,7]{2,1,3,0:T(8,128)S(1)}, f32[4,2048,128,7]{2,1,3,0:T(8,128)}, u32[]{:S(2)}) %copy-start.2) | copy-done | bytes 29360152
  86.2 8.3 %fusion.5 = bf16[128,4,7,2048]{0,3,2,1:T(8,128)(2,1)} fusion(f32[4,2048,128,7]{2,1,3,0:T(8,128)S(1)} %copy-done.2, f32[128,4,7]{0,2,1:T(8,128)S(1)} %log_add_fusion), kind=kLoop, calls=%fused_computation.9 | loop fusion | flops 22020096 | bytes 44054528 | tf_op jit(solution)/shard_map/while/body/eval_jaxpr/convert_element_type | solution.py:33
  94.6 9.3 %fusion.15 = (f32[128,4,7]{0,2,1:T(8,128)S(1)}, bf16[4,128,128,7]{2,1,3,0:T(8,128)(2,1)}) fusion(bf16[128,4,7,128]{0,3,2,1:T(8,128)(2,1)S(1)} %bitcast.100, bf16[128,4,7,2048]{0,3,2,1:T(8,128)(2,1)} %fusion.5, bf16[2048,4,128]{0,2,1:T(8,128)(2,1)} %all-gather.3.cloned.1.call-done), kind=kOutput, calls=%fused_computation.27 | convolution fusion | flops 1881338368 | bytes 18626560 | tf_op jit(solution)/shard_map/while/body/eval_jaxpr/thju,uhd->thjd/dot_general | solution.py:34
  103.8 10.7 %fusion.1 = bf16[128,4,7,2048]{0,3,2,1:T(8,128)(2,1)} fusion(bf16[128,4,7,2048]{0,3,2,1:T(8,128)(2,1)} %fusion.5, bf16[128,4,7,128]{0,3,2,1:T(8,128)(2,1)S(1)} %bitcast.101, f32[128,4,7]{0,2,1:T(8,128)S(1)} %get-tuple-element.32, bf16[2048,4,128]{0,2,1:T(8,128)(2,1)S(1)} %copy-done.4), kind=kOutput, calls=%fused_computation.2 | convolution fusion | flops 1908408320 | bytes 32389120 | tf_op jit(solution)/shard_map/while/body/eval_jaxpr/thjd,uhd->thju/dot_general | solution.py:50
  114.5 12.0 %fusion.7 = f32[2048,4,128]{0,2,1:T(8,128)} fusion(bf16[128,4,7,128]{0,3,2,1:T(8,128)(2,1)S(1)} %bitcast.104, bf16[128,4,7,2048]{0,3,2,1:T(8,128)(2,1)} %fusion.1), kind=kOutput, calls=%fused_computation.17 | convolution fusion | flops 1880096768 | bytes 19791872 | tf_op jit(solution)/shard_map/while/body/eval_jaxpr/thju,thjd->uhd/dot_general | solution.py:53
  126.6 11.8 %convolution_bitcast_fusion = f32[2048,4,128]{0,2,1:T(8,128)} fusion(bf16[128,4,7,128]{0,3,2,1:T(8,128)(2,1)S(1)} %bitcast.102, bf16[128,4,7,2048]{0,3,2,1:T(8,128)(2,1)} %fusion.5), kind=kOutput, calls=%fused_computation.18 | convolution fusion | flops 1879048192 | bytes 19791872 | tf_op jit(solution)/shard_map/while/body/eval_jaxpr/thju,thjd->uhd/dot_general | solution.py:54
  138.5 1.5 copy-done.3
  140.0 7.6 %multiply_convert_fusion = bf16[4,128,128,7]{2,1,3,0:T(8,128)(2,1)S(1)} fusion(bf16[128,4,7,2048]{0,3,2,1:T(8,128)(2,1)} %fusion.1, bf16[2048,4,128]{2,0,1:T(8,128)(2,1)S(1)} %copy-done.3), kind=kOutput, calls=%fused_computation.28 | convolution fusion | flops 1879965696 | bytes 17694720 | tf_op jit(solution)/shard_map/while/body/eval_jaxpr/thju,uhd->thjd/dot_general | solution.py:52
  147.6 14.9 %fusion.22 = f32[128,3584]{1,0:T(8,128)} fusion(bf16[128,3584]{0,1:T(8,128)(2,1)S(1)} %bitcast.105, bf16[3584,3584]{1,0:T(8,128)(2,1)} %param.8), kind=kOutput, calls=%fused_computation.36 | convolution fusion | flops 3288334336 | bytes 28442624 | tf_op jit(solution)/shard_map/tc,ec->te/dot_general | solution.py:86
  162.5 11.2 %convolution_convert_fusion.1 = bf16[128,3584]{1,0:T(8,128)(2,1)} fusion(bf16[128,3584]{0,1:T(8,128)(2,1)S(1)} %bitcast.106, bf16[3584,3584]{1,0:T(8,128)(2,1)} %param.11), kind=kOutput, calls=%fused_computation.14 | convolution fusion | flops 3288793088 | bytes 27525120 | tf_op jit(solution)/shard_map/dot_general | solution.py:23
  173.7 8.1 %reduce-scatter.3.cloned.1.call-done = f32[128,4,128]{0,2,1:T(8,128)} async-done(((f32[2048,4,128]{0,2,1:T(8,128)}), f32[128,4,128]{0,2,1:T(8,128)}) %reduce-scatter.3.cloned.1.call-update) | async-done | bytes 262160 | tf_op jit(solution)/shard_map/reduce_scatter | solution.py:84
  181.8 1.0 convert_element_type.64
  182.8 4.0 %convolution_add_fusion.1 = f32[128,3584]{1,0:T(8,128)S(1)} fusion(f32[128,3584]{1,0:T(8,128)} %fusion.22, bf16[128,512]{0,1:T(8,128)(2,1)S(1)} %bitcast.107, bf16[3584,512]{1,0:T(8,128)(2,1)} %param.9), kind=kOutput, calls=%fused_computation.11 | convolution fusion | flops 470220800 | bytes 7471104 | tf_op jit(solution)/shard_map/tc,ec->te/dot_general | solution.py:87
  186.8 55.9 %reduce-scatter.5.cloned.1.call-done = f32[128,4,128]{0,2,1:T(8,128)} async-done(((f32[2048,4,128]{0,2,1:T(8,128)}), f32[128,4,128]{0,2,1:T(8,128)}) %reduce-scatter.5.cloned.1.call-update) | async-done | bytes 262160 | tf_op jit(solution)/shard_map/reduce_scatter | solution.py:85
  242.7 1.0 convert_element_type.65
  243.7 4.3 %fusion.6 = bf16[128,3584]{1,0:T(8,128)(2,1)} fusion(f32[128,3584]{1,0:T(8,128)S(1)} %convolution_add_fusion.1, bf16[128,512]{0,1:T(8,128)(2,1)S(1)} %bitcast.108, bf16[3584,512]{1,0:T(8,128)(2,1)} %param.10), kind=kOutput, calls=%fused_computation.12 | convolution fusion | flops 470679552 | bytes 6553600 | tf_op jit(solution)/shard_map/tc,ec->te/dot_general | solution.py:88
  (24 shorter events, 3.4 us)
Async XLA Ops:
  7.2 1.2 copy-start
  7.2 46.0 %all-gather.5.cloned.1.call-start = ((), (), s32[]{:S(2)}) async-start(), calls=%async_computation.3 | async-start | bytes 2228224 | tf_op jit(solution)/shard_map/all_gather | solution.py:77
  11.8 82.8 %all-gather.3.cloned.1.call-start = ((), (), s32[]{:S(2)}) async-start(), calls=%async_computation.2 | async-start | bytes 2228224 | tf_op jit(solution)/shard_map/all_gather | solution.py:78
  15.4 166.4 %reduce-scatter.3.cloned.1.call-start = ((), (), s32[]{:S(2)}) async-start(), calls=%async_computation.4 | async-start | bytes 4456448 | tf_op jit(solution)/shard_map/reduce_scatter | solution.py:84
  68.5 17.8 %copy-start.2 = (f32[4,2048,128,7]{2,1,3,0:T(8,128)S(1)}, f32[4,2048,128,7]{2,1,3,0:T(8,128)}, u32[]{:S(2)}) copy-start(f32[4,2048,128,7]{2,1,3,0:T(8,128)} %get-tuple-element.31) | copy-start | bytes 88080384
  94.6 9.3 %copy-start.4 = (bf16[2048,4,128]{0,2,1:T(8,128)(2,1)S(1)}, bf16[2048,4,128]{0,2,1:T(8,128)(2,1)}, u32[]{:S(2)}) copy-start(bf16[2048,4,128]{0,2,1:T(8,128)(2,1)} %all-gather.3.cloned.1.call-done) | copy-start | bytes 6291460
  126.5 116.2 %reduce-scatter.5.cloned.1.call-start = ((), (), s32[]{:S(2)}) async-start(), calls=%async_computation.5 | async-start | bytes 4456448 | tf_op jit(solution)/shard_map/reduce_scatter | solution.py:85
  138.4 1.6 copy-start.3
  147.6 14.9 %copy-start.5 = (bf16[4,128,128,7]{2,1,3,0:T(8,128)(2,1)S(1)}, bf16[4,128,128,7]{2,1,3,0:T(8,128)(2,1)}, u32[]{:S(2)}) copy-start(bf16[4,128,128,7]{2,1,3,0:T(8,128)(2,1)} %get-tuple-element.33) | copy-start | bytes 2752516
  182.8 65.3 %copy-start.1 = (bf16[128,3584]{1,0:T(8,128)(2,1)S(1)}, bf16[128,3584]{1,0:T(8,128)(2,1)}, u32[]{:S(2)}) copy-start(bf16[128,3584]{1,0:T(8,128)(2,1)} %param.6) | copy-start | bytes 2752516
Sparse Core Ops, SparseCore 0:
  11.9 41.2 all-gather.4
  55.4 35.8 all-gather.2
  126.6 55.1 reduce-scatter.2
  184.0 58.6 reduce-scatter.4
where the time goes:
time: 257 us; the launch traced here: 255 us
  matrix products  131 us (51%)
  waiting for transfers between devices  75.6 us (29%)
  other arithmetic  23 us (9%)
  between operations  13.9 us (5%)
  local copies, waits for them, and re-layouts  10.6 us (4%)
    reduce_scatter x1, waiting for transfers between devices, local_body(): lax.psum_scatter(dv_part, 'cp', scatter_dimension=0, tiled=True)  55.9 us
    dot_general x4, matrix products, project(): jnp.dot(rows_in, weight, preferred_element_type=jnp.float32)  28.4 us
    dot_general x1, matrix products, one_block(): jnp.einsum('thjd,uhd->thju', q_blk, k_all, preferred_element_type=jnp.flo...  15.2 us
    dot_general x1, matrix products, local_body(): jnp.einsum('tc,ec->te', dq_flat, w_q, preferred_element_type=jnp.float32)  14.9 us
    dot_general x1, matrix products, local_body(): jnp.einsum('te,ce->tc', dy_loc, w_o, preferred_element_type=jnp.float32)  13.1 us
    reduce_sum x1, other arithmetic, one_block(): lse_blk = jax.nn.logsumexp(scores, axis=-1, keepdims=True)  12.7 us
    dot_general x1, matrix products, one_block(): jnp.einsum('thju,thjd->uhd', dscore, q_blk, preferred_element_type=jnp.fl...  12 us
    dot_general x1, matrix products, one_block(): jnp.einsum('thju,thjd->uhd', prob_bf, do_blk, preferred_element_type=jnp....  11.8 us
  transfers between devices with their start and end apart: 4, of which 3 were waited for; matrix products, arithmetic and copies ran while one was open for 46% of the time, Pallas kernels for 0%

commit v1 on v0

v1 whole, which is shorter than its diff:
```python
import functools
import math

import jax
import jax.numpy as jnp
from jax import lax
from jax.experimental import pallas as pl
from jax.experimental.pallas import tpu as pltpu
from jax.sharding import PartitionSpec as P

HEAD_DIM = 128
MESH = pl.DeviceIdType.MESH
BF = jnp.bfloat16
F32 = jnp.float32
UP, DOWN = 0, 1


def mm(a, b):
    return jnp.dot(a, b, preferred_element_type=F32)


def mm_nt(a, b):
    return lax.dot_general(a, b, (((1,), (1,)), ((), ())), preferred_element_type=F32)


def layer_kernel(n_dev, kv_heads, q_group,
                 x_hbm, dy_hbm, wq_hbm, wk_hbm, wv_hbm, wo_hbm, y_hbm, dx_hbm,
                 x_v, dy_v, wq_v, wo_v, kv_v, kt_v, vt_v, q_v, do_v, qt_v, dot_v, o_v, dq_v,
                 s_v, p_v, ds_v, part_v, pre_v, ring_v, yacc_v, dxacc_v, fin_v, fout_v,
                 in_sem, w_sem, slab_sem, ag_send, ag_recv, pre_send, pre_recv, rs_send, rs_recv,
                 fin_send, fin_recv, out_sem):
    n_chip = n_dev // 2
    far = n_chip // 2
    tok = x_v.shape[0]
    width = x_v.shape[1]
    hd = HEAD_DIM
    gcol = q_group * hd
    kvcol = kv_heads * hd
    n_piece = width // gcol
    scale = hd ** -0.5
    scale2 = scale * math.log2(math.e)

    me = lax.axis_index("cp")
    core = lax.rem(me, 2)
    chip = me // 2
    mate = me + 1 - 2 * core

    def chip_at(off):
        return lax.rem(chip + off + n_chip, n_chip)

    near = (2 * chip_at(1) + core, 2 * chip_at(-1) + core)

    def remote(src, dst, ssem, rsem, dev):
        return pltpu.make_async_remote_copy(src_ref=src, dst_ref=dst, send_sem=ssem, recv_sem=rsem,
                                            device_id={"cp": dev}, device_id_type=MESH)

    def small_copies(hbm, buf, base):
        out = []
        for b in range(n_piece):
            out.append(pltpu.make_async_copy(hbm.at[pl.ds(b * gcol, gcol), :],
                                             buf.at[:, pl.ds(b * kvcol, kvcol)], w_sem.at[base + b]))
        return out

    def slab_copies(h, slot):
        col = h * gcol if isinstance(h, int) else pl.multiple_of(h * gcol, 128)
        return (pltpu.make_async_copy(wq_hbm.at[:, pl.ds(col, gcol)], wq_v.at[slot], slab_sem.at[slot, 0]),
                pltpu.make_async_copy(wo_hbm.at[pl.ds(col, gcol), :], wo_v.at[slot], slab_sem.at[slot, 1]))

    def src_chip(d, hop):
        return chip_at(-hop) if d == UP else chip_at(hop)

    def ag_view(h, dev, d, hop):
        if hop < far:
            return kv_v.at[h, dev]
        return kv_v.at[h, dev, d]

    def ag_ring(h, d, hop):
        ref = ag_view(h, 2 * src_chip(d, hop) + core, d, hop)
        ssem = ag_send.at[h, d] if hop == 1 else ag_send.at[h, 3 + d * (far - 1) + hop - 2]
        return remote(ref, ref, ssem, ag_recv.at[h, d * far + hop - 1], near[d])

    def ag_ring_out(h, d, hop):
        dev = me if hop == 1 else 2 * src_chip(d, hop - 1) + core
        ref = ag_view(h, dev, d, hop)
        ssem = ag_send.at[h, d] if hop == 1 else ag_send.at[h, 3 + d * (far - 1) + hop - 2]
        return remote(ref, ref, ssem, ag_recv.at[h, d * far + hop - 1], near[d])

    def ag_mate_own(h):
        ref = kv_v.at[h, me]
        return remote(ref, ref, ag_send.at[h, 2], ag_recv.at[h, 2 * far], mate)

    def ag_mate_out(h, d, hop):
        ref = ag_view(h, 2 * src_chip(d, hop) + core, d, hop)
        idx = 2 * far + 1 + d * far + hop - 1
        return remote(ref, ref, ag_send.at[h, idx], ag_recv.at[h, idx], mate)

    def ag_mate_in(h, d, hop):
        ref = ag_view(h, 2 * src_chip(d, hop) + 1 - core, d, hop)
        idx = 2 * far + 1 + d * far + hop - 1
        return remote(ref, ref, ag_send.at[h, idx], ag_recv.at[h, idx], mate)

    def ag_start(h):
        for d in (UP, DOWN):
            ag_ring_out(h, d, 1).start()
        ag_mate_own(h).start()

    def ag_level(h, hop):
        for d in (UP, DOWN):
            ag_ring(h, d, hop).wait_recv()
            if hop < far:
                ag_ring_out(h, d, hop + 1).start()
            ag_mate_out(h, d, hop).start()

    def ag_finish(h):
        ref = kv_v.at[h, mate]
        remote(ref, ref, ag_send.at[h, 2], ag_recv.at[h, 2 * far], mate).wait_recv()
        for hop in range(1, far + 1):
            for d in (UP, DOWN):
                ag_mate_in(h, d, hop).wait_recv()

    def ag_drain(h):
        ag_mate_own(h).wait_send()
        for d in (UP, DOWN):
            for hop in range(1, far + 1):
                ag_ring_out(h, d, hop).wait_send()
                ag_mate_out(h, d, hop).wait_send()

    def pre_copy(h, c):
        slot = lax.rem(h, 2)
        return remote(part_v.at[slot, 1 - core, pl.ds(2 * c, 2)], pre_v.at[slot, pl.ds(2 * c, 2)],
                      pre_send.at[h, c], pre_recv.at[h, c], mate)

    def chain_len(ch):
        return far - ch

    def rs_index(ch, lvl):
        return lvl if ch == 0 else far + lvl

    def rs_dest(d, ch, lvl):
        dist = chain_len(ch) - lvl
        to = chip_at(dist) if d == UP else chip_at(-dist)
        half = ch if d == UP else 1 - ch
        return 2 * to + half

    def rs_copy(h, d, ch, lvl):
        slot = lax.rem(h, 2)
        i = rs_index(ch, lvl)
        src = part_v.at[slot, core, rs_dest(d, ch, 0)] if lvl == 0 else ring_v.at[h, d, rs_index(ch, lvl - 1)]
        return remote(src, ring_v.at[h, d, i], rs_send.at[h, d, i], rs_recv.at[h, d, i], near[d])

    def rs_begin(h):
        slot = lax.rem(h, 2)
        for c in range(n_chip):
            pre_copy(h, c).wait()
        for e in range(n_dev):
            part_v[slot, core, e] = part_v[slot, core, e] + pre_v[slot, e]
        for d in (UP, DOWN):
            for ch in (0, 1):
                rs_copy(h, d, ch, 0).start()

    def rs_level(h, lvl):
        slot = lax.rem(h, 2)
        for ch in (0, 1):
            if lvl < chain_len(ch):
                for d in (UP, DOWN):
                    rs_copy(h, d, ch, lvl - 1).wait_recv()
                    i = rs_index(ch, lvl - 1)
                    ring_v[h, d, i] = ring_v[h, d, i] + part_v[slot, core, rs_dest(d, ch, lvl)]
                    rs_copy(h, d, ch, lvl).start()

    def fin_copy(h):
        return remote(fout_v.at[h], fin_v.at[core, h], fin_send.at[h], fin_recv.at[h], mate)

    def rs_end(h):
        slot = lax.rem(h, 2)
        for ch in (0, 1):
            for d in (UP, DOWN):
                rs_copy(h, d, ch, chain_len(ch) - 1).wait_recv()
        factor = jnp.where(core == 0, scale, 1.0).astype(F32)
        for half in (0, 1):
            up = ring_v[h, UP, rs_index(half, chain_len(half) - 1)]
            dn = ring_v[h, DOWN, rs_index(1 - half, chain_len(1 - half) - 1)]
            total = (part_v[slot, core, 2 * chip + half] + up + dn) * factor
            done = total.astype(BF)

            @pl.when(core == half)
            def _():
                fin_v[core, h] = done

            @pl.when(core != half)
            def _():
                fout_v[h] = done
        fin_copy(h).start()
        for ch in (0, 1):
            for lvl in range(chain_len(ch)):
                for d in (UP, DOWN):
                    rs_copy(h, d, ch, lvl).wait_send()

    def project_q(slot):
        q = mm(x_v[...], wq_v[slot]).astype(BF)
        q_v[slot] = q

    def project_do(slot):
        do_v[slot] = mm_nt(dy_v[...], wo_v[slot]).astype(BF)

    def transpose_kv(h):
        for e in range(n_dev):
            kt_v[:, e * tok:(e + 1) * tok] = kv_v[h, e, 0].T
            vt_v[:, e * tok:(e + 1) * tok] = kv_v[h, e, 1].T

    n_key = n_dev * tok
    chunk = 2 * tok

    def stage_scores(slot, j):
        cols = slice(j * hd, (j + 1) * hd)
        q_j = q_v[slot, :, cols]
        qt_v[:, cols] = q_j.T
        dot_v[:, cols] = do_v[slot, :, cols].T
        part_max = None
        for n in range(n_key // chunk):
            s = mm(q_j, kt_v[:, n * chunk:(n + 1) * chunk]) * scale2
            s_v[:, n * chunk:(n + 1) * chunk] = s
            for i in range(chunk // 128):
                piece = s[:, i * 128:(i + 1) * 128]
                part_max = piece if part_max is None else jnp.maximum(part_max, piece)
        row_max = jnp.max(part_max, axis=1, keepdims=True)
        for r in range(0, tok, 16):
            e = jnp.exp2(s_v[r:r + 16, :] - row_max[r:r + 16])
            total = jnp.sum(e, axis=1, keepdims=True)
            p_v[j * tok + r:j * tok + r + 16, :] = (e * (1.0 / total)).astype(BF)

    def stage_grads(h, slot, j):
        cols = slice(j * hd, (j + 1) * hd)
        rows = slice(j * tok, (j + 1) * tok)
        v_all = kv_v[h, :, 1].reshape(n_key, hd)
        out = mm(p_v[rows, :], v_all).astype(BF)
        o_v[slot, :, cols] = out
        do_j = do_v[slot, :, cols]
        delta = jnp.sum(out.astype(F32) * do_j.astype(F32), axis=1, keepdims=True)
        for n in range(n_key // chunk):
            kc = slice(n * chunk, (n + 1) * chunk)
            dp = mm(do_j, vt_v[:, kc])
            ds_v[rows, kc] = (p_v[rows, kc].astype(F32) * (dp - delta)).astype(BF)
        k_all = kv_v[h, :, 0].reshape(n_key, hd)
        dq_v[slot, :, cols] = (mm(ds_v[rows, :], k_all) * scale).astype(BF)

    def key_grads(h):
        slot = lax.rem(h, 2)
        for c in range(n_chip):
            kc = slice(c * chunk, (c + 1) * chunk)
            gk = mm(qt_v[...], ds_v[:, kc])
            gv = mm(dot_v[...], p_v[:, kc])
            for half in (0, 1):
                part_v[slot, 0, 2 * c + half] = gk[:, half * tok:(half + 1) * tok]
                part_v[slot, 1, 2 * c + half] = gv[:, half * tok:(half + 1) * tok]
            pre_copy(h, c).start()

    def outputs_y(slot):
        for b in range(n_piece):
            cols = slice(b * gcol, (b + 1) * gcol)
            yacc_v[:, cols] += mm(o_v[slot], wo_v[slot, :, cols])

    def outputs_dx(slot):
        for b in range(n_piece):
            cols = slice(b * gcol, (b + 1) * gcol)
            dxacc_v[:, cols] += mm_nt(dq_v[slot], wq_v[slot, cols, :])

    x_copy = pltpu.make_async_copy(x_hbm, x_v, in_sem.at[0])
    dy_copy = pltpu.make_async_copy(dy_hbm, dy_v, in_sem.at[1])
    x_copy.start()
    wk_in = small_copies(wk_hbm, p_v, 0)
    wv_in = small_copies(wv_hbm, ds_v, n_piece)
    for copy in wk_in + wv_in:
        copy.start()

    barrier = pltpu.get_barrier_semaphore()
    for dev in (near[UP], near[DOWN], mate):
        pl.semaphore_signal(barrier, inc=1, device_id={"cp": dev}, device_id_type=MESH)

    yacc_v[...] = jnp.zeros_like(yacc_v)
    dxacc_v[...] = jnp.zeros_like(dxacc_v)
    x_copy.wait()

    def project_small(copies, buf, which):
        acc = None
        for b in range(n_piece):
            copies[b].wait()
            term = mm(x_v[:, b * gcol:(b + 1) * gcol], buf[:, b * kvcol:(b + 1) * kvcol])
            acc = term if acc is None else acc + term
        acc = acc.astype(BF)
        for h in range(kv_heads):
            kv_v[h, me, which] = acc[:, h * hd:(h + 1) * hd]

    project_small(wk_in, p_v, 0)
    for copy in slab_copies(0, 0):
        copy.start()
    dy_copy.start()
    project_small(wv_in, ds_v, 1)
    pl.semaphore_wait(barrier, 3)
    for h in (0, 1):
        ag_start(h)
    for copy in slab_copies(1, 1):
        copy.start()
    dy_copy.wait()
    slab_copies(0, 0)[0].wait()
    project_q(0)
    for h in (0, 1):
        ag_level(h, 1)
    slab_copies(0, 0)[1].wait()
    project_do(0)
    for h in (0, 1):
        ag_level(h, 2)
    slab_copies(1, 1)[0].wait()
    project_q(1)
    for h in (0, 1):
        ag_level(h, 3)
    for h in range(2, kv_heads):
        ag_start(h)
    slab_copies(1, 1)[1].wait()
    project_do(1)
    for h in (0, 1):
        ag_level(h, 4)

    def head_step(h, carry):
        slot = lax.rem(h, 2)
        ag_finish(h)
        transpose_kv(h)
        stage_scores(slot, 0)
        for j in range(q_group):
            if j in (0, 2, 4, 6):
                @pl.when(h == 0)
                def _():
                    for g in range(2, kv_heads):
                        ag_level(g, j // 2 + 1)
            if j in (0, 3, 6):
                @pl.when(h >= 1)
                def _():
                    rs_level(h - 1, j // 3 + 1)
            if j == 1:
                @pl.when(h >= 2)
                def _():
                    rs_end(h - 2)
            if j + 1 < q_group:
                stage_scores(slot, j + 1)
            stage_grads(h, slot, j)
        key_grads(h)

        @pl.when(h + 2 < kv_heads)
        def _():
            outputs_y(slot)
            outputs_dx(slot)
            for copy in slab_copies(h + 2, slot):
                copy.start()

        rs_begin(h)

        @pl.when((h >= 1) & (h + 1 < kv_heads))
        def _():
            for copy in slab_copies(h + 1, 1 - slot):
                copy.wait()
            project_q(1 - slot)
            project_do(1 - slot)

        return carry

    lax.fori_loop(0, kv_heads, head_step, 0)

    last = kv_heads - 1
    wk_in = small_copies(wk_hbm, p_v, 0)
    wv_in = small_copies(wv_hbm, ds_v, n_piece)
    for copy in wk_in + wv_in:
        copy.start()
    slot_a, slot_b = (last - 1) % 2, last % 2
    outputs_y(slot_a)
    rs_level(last, 1)
    rs_end(last - 1)
    outputs_dx(slot_a)
    rs_level(last, 2)
    outputs_y(slot_b)
    rs_level(last, 3)
    x_v[...] = yacc_v[...].astype(BF)
    y_copy = pltpu.make_async_copy(x_v, y_hbm, out_sem.at[0])
    y_copy.start()
    outputs_dx(slot_b)
    rs_end(last)
    for h in range(kv_heads):
        remote(fout_v.at[h], fin_v.at[1 - core, h], fin_send.at[h], fin_recv.at[h], mate).wait_recv()
    for copy in wk_in + wv_in:
        copy.wait()
    gk = jnp.concatenate([fin_v[0, h].T for h in range(kv_heads)], axis=1)
    gv = jnp.concatenate([fin_v[1, h].T for h in range(kv_heads)], axis=1)
    for b in range(n_piece):
        cols = slice(b * gcol, (b + 1) * gcol)
        kcols = slice(b * kvcol, (b + 1) * kvcol)
        total = dxacc_v[:, cols] + mm_nt(gk, p_v[:, kcols]) + mm_nt(gv, ds_v[:, kcols])
        dy_v[:, cols] = total.astype(BF)
    dx_copy = pltpu.make_async_copy(dy_v, dx_hbm, out_sem.at[1])
    dx_copy.start()
    for h in range(kv_heads):
        ag_drain(h)
        fin_copy(h).wait_send()
    y_copy.wait()
    dx_copy.wait()


def solution(mesh):
    n_dev = mesh.shape["cp"]
    row_spec = P(("dp", "cp"), None)
    full_spec = P(None, None)

    def local_body(x_loc, dy_loc, w_q, w_k, w_v, w_o):
        tok, width = x_loc.shape
        q_heads = w_q.shape[1] // HEAD_DIM
        kv_heads = w_k.shape[1] // HEAD_DIM
        q_group = q_heads // kv_heads
        gcol = q_group * HEAD_DIM
        n_key = tok * n_dev
        far = n_dev // 4
        hd = HEAD_DIM
        any_spec = pl.BlockSpec(memory_space=pl.ANY)
        dma = pltpu.SemaphoreType.DMA
        scratch = [
            pltpu.VMEM((tok, width), BF), pltpu.VMEM((tok, width), BF),
            pltpu.VMEM((2, width, gcol), BF), pltpu.VMEM((2, gcol, width), BF),
            pltpu.VMEM((kv_heads, n_dev, 2, tok, hd), BF),
            pltpu.VMEM((hd, n_key), BF), pltpu.VMEM((hd, n_key), BF),
            pltpu.VMEM((2, tok, gcol), BF), pltpu.VMEM((2, tok, gcol), BF),
            pltpu.VMEM((hd, q_group * tok), BF), pltpu.VMEM((hd, q_group * tok), BF),
            pltpu.VMEM((2, tok, gcol), BF), pltpu.VMEM((2, tok, gcol), BF),
            pltpu.VMEM((tok, n_key), F32),
            pltpu.VMEM((q_group * tok, n_key), BF), pltpu.VMEM((q_group * tok, n_key), BF),
            pltpu.VMEM((2, 2, n_dev, hd, tok), F32), pltpu.VMEM((2, n_dev, hd, tok), F32),
            pltpu.VMEM((kv_heads, 2, 2 * far - 1, hd, tok), F32),
            pltpu.VMEM((tok, width), F32), pltpu.VMEM((tok, width), F32),
            pltpu.VMEM((2, kv_heads, hd, tok), BF), pltpu.VMEM((kv_heads, hd, tok), BF),
            dma((2,)), dma((2 * (width // gcol),)), dma((2, 2)),
            dma((kv_heads, 4 * far + 1)), dma((kv_heads, 4 * far + 1)),
            dma((kv_heads, n_dev // 2)), dma((kv_heads, n_dev // 2)),
            dma((kv_heads, 2, 2 * far - 1)), dma((kv_heads, 2, 2 * far - 1)),
            dma((kv_heads,)), dma((kv_heads,)), dma((2,)),
        ]
        out = jax.ShapeDtypeStruct((tok, width), BF)
        return pl.pallas_call(
            functools.partial(layer_kernel, n_dev, kv_heads, q_group),
            out_shape=(out, out),
            in_specs=[any_spec] * 6,
            out_specs=(any_spec, any_spec),
            scratch_shapes=scratch,
            name="layer",
            compiler_params=pltpu.CompilerParams(collective_id=0, has_side_effects=True,
                                                 vmem_limit_bytes=67043328),
        )(x_loc, dy_loc, w_q, w_k, w_v, w_o)

    return jax.shard_map(local_body, mesh=mesh,
                         in_specs=(row_spec, row_spec, full_spec, full_spec, full_spec, full_spec),
                         out_specs=(row_spec, row_spec), check_vma=False)
```

time: 257 us -> 130 us (0.51)
  matrix products: 131 us -> 0 us
  Pallas kernels: 0 us -> 125 us
  waiting for transfers between devices: 75.6 us -> 0 us
  other arithmetic: 23 us -> 0 us
  between operations: 13.9 us -> 0.64 us
  local copies, waits for them, and re-layouts: 10.6 us -> 4.32 us
    dot_general x14 -> x0, matrix products: 131 us -> none  [the longest x4 28.4 us: project(): jnp.dot(rows_in, weight, preferred_element_type=jnp.float32)]
    pallas_call x0 -> x1, Pallas kernels: none -> 125 us  [local_body(): pl.pallas_call(functools.partial(layer_kernel, n_dev, kv_heads, q_group),...]
    reduce_scatter x2 -> x0, waiting for transfers between devices: 64 us -> none  [the longest x1 55.9 us: local_body(): lax.psum_scatter(dv_part, 'cp', scatter_dimension=0, tiled=True)]
    reduce_sum x1 -> x0, other arithmetic: 12.7 us -> none  [one_block(): lse_blk = jax.nn.logsumexp(scores, axis=-1, keepdims=True)]
    all_gather x2 -> x0, waiting for transfers between devices: 11.4 us -> none  [the longest x1 11.4 us: local_body(): k_all = lax.all_gather(k_loc, 'cp', axis=0, tiled=True)]
    convert_element_type x3 -> x0, other arithmetic: 10.3 us -> none  [the longest x1 8.33 us: one_block(): prob_bf = jnp.exp(scores - lse_blk).astype(jnp.bfloat16)]
    unnamed x12 -> x2, local copies, waits for them, and re-layouts: 7.7 us -> 4.32 us
  transfers between devices with their start and end apart: 4 -> 0, of which waited for: 3 -> 0; matrix products, arithmetic and copies ran while one was open for 46% -> 0% of each run, Pallas kernels for 0% -> 0%
where the time goes in v1:
time: 130 us
  Pallas kernels  125 us (96%)
  local copies, waits for them, and re-layouts  4.32 us (3%)
    pallas_call x1, Pallas kernels, local_body(): pl.pallas_call(functools.partial(layer_kernel, n_dev, kv_heads, q_group),...  125 us
    unnamed x2, local copies, waits for them, and re-layouts  4.32 us

profile of v1, /device:TPU:21, one launch (start us, length us, event | category | flops | bytes accessed | tf_op | source)
XLA Modules:
  0.0 129.8 jit_solution(6101196919601184005)
XLA Ops:
  0.6 124.8 %layer.1 = (bf16[128,3584]{1,0:T(8,128)(2,1)}, bf16[128,3584]{1,0:T(8,128)(2,1)}) custom-call(bf16[128,3584]{1,0:T(8,128)(2,1)} %x_hbm.1, bf16[128,3584]{1,0:T(8,128)(2,1)} %dy_hbm.1, bf16[3584,3584]{1,0:T(8,128)(2,1)} %wq_hbm.1, bf16[3584,512]{1,0:T(8,128)(2,1)} %wk_hbm.1, bf16[3584,512]{1,0:T(8,128)(2,1)} %wv_hbm.1, bf16[3584,3584]{1,0:T(8,128)(2,1)} %wo_hbm.1), custom_call_target="tpu_custom_call" | custom-call | tf_op jit(solution)/shard_map/layer/pallas_call | solution.py:443
  125.4 2.2 %copy.10 = bf16[128,3584]{1,0:T(8,128)(2,1)} copy(bf16[128,3584]{1,0:T(8,128)(2,1)} %get-tuple-element.4) | data formatting | bytes 1835008
  127.6 2.2 %copy.11 = bf16[128,3584]{1,0:T(8,128)(2,1)} copy(bf16[128,3584]{1,0:T(8,128)(2,1)} %get-tuple-element.5) | data formatting | bytes 1835008

commit v2 on v1

v2 whole, which is shorter than its diff:
```python
import functools
import math

import jax
import jax.numpy as jnp
from jax import lax
from jax.experimental import pallas as pl
from jax.experimental.pallas import tpu as pltpu
from jax.sharding import PartitionSpec as P

HEAD_DIM = 128
MESH = pl.DeviceIdType.MESH
BF = jnp.bfloat16
F32 = jnp.float32
UP, DOWN = 0, 1


def mm(a, b):
    return jnp.dot(a, b, preferred_element_type=F32)


def mm_nt(a, b):
    return lax.dot_general(a, b, (((1,), (1,)), ((), ())), preferred_element_type=F32)


def layer_kernel(n_dev, kv_heads, q_group,
                 x_hbm, dy_hbm, wq_hbm, wk_hbm, wv_hbm, wo_hbm, y_hbm, dx_hbm,
                 x_v, dy_v, wq_v, wo_v, kv_v, kt_v, vt_v, q_v, do_v, qt_v, dot_v,
                 s_v, p_v, ds_v, part_v, pre_v, ring_v, yacc_v, dxacc_v, fin_v, fout_v,
                 in_sem, w_sem, slab_sem, ag_send, ag_recv, pre_send, pre_recv, rs_send, rs_recv,
                 fin_send, fin_recv, out_sem):
    n_chip = n_dev // 2
    far = n_chip // 2
    tok = x_v.shape[0]
    width = x_v.shape[1]
    hd = HEAD_DIM
    gcol = q_group * hd
    kvcol = kv_heads * hd
    n_piece = width // gcol
    n_key = n_dev * tok
    chunk = 2 * tok
    scale = hd ** -0.5
    scale2 = scale * math.log2(math.e)

    me = lax.axis_index("cp")
    core = lax.rem(me, 2)
    chip = me // 2
    mate = me + 1 - 2 * core

    def chip_at(off):
        return lax.rem(chip + off + n_chip, n_chip)

    near = (2 * chip_at(1) + core, 2 * chip_at(-1) + core)

    def remote(src, dst, ssem, rsem, dev):
        return pltpu.make_async_remote_copy(src_ref=src, dst_ref=dst, send_sem=ssem, recv_sem=rsem,
                                            device_id={"cp": dev}, device_id_type=MESH)

    def small_copies(hbm, buf, base):
        return [pltpu.make_async_copy(hbm.at[pl.ds((i // 2) * gcol, gcol), pl.ds((i % 2) * chunk, chunk)],
                                      buf.at[i], w_sem.at[base + i]) for i in range(n_chip)]

    def col_of(h):
        return h * gcol if isinstance(h, int) else pl.multiple_of(h * gcol, 128)

    def slab_q(h, slot):
        return pltpu.make_async_copy(wq_hbm.at[:, pl.ds(col_of(h), gcol)], wq_v.at[slot], slab_sem.at[slot, 0])

    def slab_o(h, slot):
        return pltpu.make_async_copy(wo_hbm.at[pl.ds(col_of(h), gcol), :], wo_v.at[slot], slab_sem.at[slot, 1])

    def src_chip(d, hop):
        return chip_at(-hop) if d == UP else chip_at(hop)

    def ag_view(h, dev, d, hop):
        if hop < far:
            return kv_v.at[h, dev]
        return kv_v.at[h, dev, d]

    def ag_ring(h, d, hop):
        ref = ag_view(h, 2 * src_chip(d, hop) + core, d, hop)
        return remote(ref, ref, ag_send.at[h], ag_recv.at[h, d * far + hop - 1], near[d])

    def ag_ring_out(h, d, hop):
        dev = me if hop == 1 else 2 * src_chip(d, hop - 1) + core
        ref = ag_view(h, dev, d, hop)
        return remote(ref, ref, ag_send.at[h], ag_recv.at[h, d * far + hop - 1], near[d])

    def ag_mate_own(h):
        ref = kv_v.at[h, me]
        return remote(ref, ref, ag_send.at[h], ag_recv.at[h, 2 * far], mate)

    def ag_mate_out(h, d, hop):
        ref = ag_view(h, 2 * src_chip(d, hop) + core, d, hop)
        idx = 2 * far + 1 + d * far + hop - 1
        return remote(ref, ref, ag_send.at[h], ag_recv.at[h, idx], mate)

    def ag_mate_in(h, d, hop):
        ref = ag_view(h, 2 * src_chip(d, hop) + 1 - core, d, hop)
        idx = 2 * far + 1 + d * far + hop - 1
        return remote(ref, ref, ag_send.at[h], ag_recv.at[h, idx], mate)

    def ag_start(h):
        for d in (UP, DOWN):
            ag_ring_out(h, d, 1).start()
        ag_mate_own(h).start()

    def ag_level(h, hop):
        for d in (UP, DOWN):
            ag_ring(h, d, hop).wait_recv()
            if hop < far:
                ag_ring_out(h, d, hop + 1).start()
            ag_mate_out(h, d, hop).start()

    def ag_finish(h):
        ref = kv_v.at[h, mate]
        remote(ref, ref, ag_send.at[h], ag_recv.at[h, 2 * far], mate).wait_recv()
        for hop in range(1, far + 1):
            for d in (UP, DOWN):
                ag_mate_in(h, d, hop).wait_recv()

    def ag_drain(h):
        ref = kv_v.at[h, pl.ds(0, n_dev - 1)]
        remote(ref, ref, ag_send.at[h], ag_recv.at[h, 0], mate).wait_send()

    def slot_of(off):
        return off % n_chip

    def pre_copy(h, off):
        slot, i = lax.rem(h, 2), slot_of(off)
        return remote(part_v.at[slot, 1 - core, i], pre_v.at[h, i], pre_send.at[h], pre_recv.at[h, i], mate)

    def chain_len(ch):
        return far - ch

    def rs_index(ch, lvl):
        return lvl if ch == 0 else far + lvl

    def rs_place(d, ch, lvl):
        dist = chain_len(ch) - lvl
        return slot_of(dist if d == UP else -dist), (ch if d == UP else 1 - ch)

    def rs_copy(h, d, ch, lvl):
        i = rs_index(ch, lvl)
        if lvl == 0:
            off, half = rs_place(d, ch, 0)
            src = part_v.at[lax.rem(h, 2), core, off, half]
        else:
            src = ring_v.at[h, d, rs_index(ch, lvl - 1)]
        return remote(src, ring_v.at[h, d, i], rs_send.at[h], rs_recv.at[h, d, i], near[d])

    def rs_begin(h):
        slot = lax.rem(h, 2)
        for off in (far, far - 1, 1 - far):
            pre_copy(h, off).wait_recv()
        for ch in (0, 1):
            for d in (UP, DOWN):
                off, half = rs_place(d, ch, 0)
                part_v[slot, core, off, half] = part_v[slot, core, off, half] + pre_v[h, off, half]
                rs_copy(h, d, ch, 0).start()

    def rs_step(h, ch, lvl):
        slot = lax.rem(h, 2)
        places = [rs_place(d, ch, lvl) for d in (UP, DOWN)]
        if ch == 1:
            for off, _ in places:
                pre_copy(h, off).wait_recv()
        mine = [part_v[slot, core, off, half] + pre_v[h, off, half] for off, half in places]
        i = rs_index(ch, lvl - 1)
        for d in (UP, DOWN):
            rs_copy(h, d, ch, lvl - 1).wait_recv()
            ring_v[h, d, i] = ring_v[h, d, i] + mine[d]
            rs_copy(h, d, ch, lvl).start()

    def fin_copy(h):
        return remote(fout_v.at[h], fin_v.at[core, h], fin_send.at[h], fin_recv.at[h], mate)

    def rs_end(h):
        slot = lax.rem(h, 2)
        pre_copy(h, 0).wait_recv()
        for ch in (0, 1):
            for d in (UP, DOWN):
                rs_copy(h, d, ch, chain_len(ch) - 1).wait_recv()
        factor = jnp.where(core == 0, scale, 1.0).astype(F32)
        for half in (0, 1):
            up = ring_v[h, UP, rs_index(half, chain_len(half) - 1)]
            dn = ring_v[h, DOWN, rs_index(1 - half, chain_len(1 - half) - 1)]
            total = (part_v[slot, core, 0, half] + pre_v[h, 0, half] + up + dn) * factor
            done = total.astype(BF)

            @pl.when(core == half)
            def _():
                fin_v[core, h] = done

            @pl.when(core != half)
            def _():
                fout_v[h] = done
        fin_copy(h).start()
        remote(ring_v.at[h], ring_v.at[h], rs_send.at[h], rs_recv.at[h, 0, 0], near[UP]).wait_send()
        remote(pre_v.at[h], pre_v.at[h], pre_send.at[h], pre_recv.at[h, 0], mate).wait_send()

    def project_q(h, slot):
        q_v[h] = mm(x_v[...], wq_v[slot]).astype(BF)

    do_cut = (gcol // 2 + chunk - 1) // chunk * chunk

    def project_do(h, slot, part):
        cols = slice(0, do_cut) if part == 0 else slice(do_cut, gcol)
        do_v[h, :, cols] = mm_nt(dy_v[...], wo_v[slot, cols, :]).astype(BF)

    def transpose_kv(h):
        for e in range(n_dev):
            c, cols = e // 2, slice((e % 2) * tok, (e % 2 + 1) * tok)
            kt_v[c, :, cols] = kv_v[h, e, 0].T
            vt_v[c, :, cols] = kv_v[h, e, 1].T

    blk = 16
    n_blk = tok // blk

    def attend(h, serve):
        row_max, delta = {}, {}

        def lanes(j):
            return slice(j * hd, (j + 1) * hd)

        def rows(j):
            return slice(j * tok, (j + 1) * tok)

        def scores(j, i, state):
            if i == 0:
                qt_v[:, lanes(j)] = q_v[h, :, lanes(j)].T
                dot_v[:, lanes(j)] = do_v[h, :, lanes(j)].T
            s = mm(q_v[h, :, lanes(j)], kt_v[i]) * scale2
            s_v[j % 2, i] = s
            top = jnp.maximum(s[:, :hd], s[:, hd:])
            state["top"] = top if i == 0 else jnp.maximum(state["top"], top)
            if i == n_chip - 1:
                row_max[j] = jnp.max(state["top"], axis=1, keepdims=True)

        def exps(j, i, state):
            r = slice(i * blk, (i + 1) * blk)
            total = None
            for c in range(n_chip):
                e = jnp.exp2(s_v[j % 2, c, r, :] - row_max[j][r])
                s_v[j % 2, c, r, :] = e
                both = e[:, :hd] + e[:, hd:]
                total = both if total is None else total + both
            state[i] = 1.0 / jnp.sum(total, axis=1, keepdims=True)

        def probs(j, i, state):
            r = slice(i * blk, (i + 1) * blk)
            for c in range(n_chip):
                p_v[c, j * tok + i * blk:j * tok + (i + 1) * blk, :] = (s_v[j % 2, c, r, :] * state[i]).astype(BF)

        def kv_chunk(i, which):
            return kv_v[h, 2 * i:2 * i + 2, which].reshape(chunk, hd)

        def add_to(state, name, term):
            state[name] = term if name not in state else state[name] + term

        for b in range(-2, q_group + 1):
            state = {}
            soft = {}
            serve(b)
            for i in range(n_chip + 1):
                if i < n_chip and 0 <= b - 1 < q_group:
                    add_to(state, "dq", mm(ds_v[i, rows(b - 1), :], kv_chunk(i, 0)))
                if i < n_chip and 0 <= b + 2 < q_group:
                    scores(b + 2, i, state)
                if 0 <= b + 1 < q_group:
                    if i < n_blk:
                        exps(b + 1, i, soft)
                    if i > 0:
                        probs(b + 1, i - 1, soft)
            if 0 <= b - 1 < q_group:
                do_v[h, :, lanes(b - 1)] = (state["dq"] * scale).astype(BF)
            for i in range(n_chip):
                if 0 <= b + 1 < q_group:
                    add_to(state, "out", mm(p_v[i, rows(b + 1), :], kv_chunk(i, 1)))
                if 0 <= b < q_group:
                    dp = mm(do_v[h, :, lanes(b)], vt_v[i])
                    ds_v[i, rows(b), :] = (p_v[i, rows(b), :].astype(F32) * (dp - delta[b])).astype(BF)
            if 0 <= b + 1 < q_group:
                out = state["out"].astype(BF)
                q_v[h, :, lanes(b + 1)] = out
                do_j = do_v[h, :, lanes(b + 1)].astype(F32)
                delta[b + 1] = jnp.sum(out.astype(F32) * do_j, axis=1, keepdims=True)

    def key_grads(h):
        slot = lax.rem(h, 2)
        order = [far]
        for dist in range(far - 1, 0, -1):
            order += [dist, -dist]
        order.append(0)
        for group in (order[:3], order[3:]):
            for off in group:
                c = chip_at(off)
                gk = mm(qt_v[...], ds_v[c])
                gv = mm(dot_v[...], p_v[c])
                for half in (0, 1):
                    part_v[slot, 0, slot_of(off), half] = gk[:, half * tok:(half + 1) * tok]
                    part_v[slot, 1, slot_of(off), half] = gv[:, half * tok:(half + 1) * tok]
            for off in group:
                pre_copy(h, off).start()

    def outputs_y(h, slot):
        for b in range(n_piece):
            cols = slice(b * gcol, (b + 1) * gcol)
            yacc_v[:, cols] += mm(q_v[h], wo_v[slot, :, cols])

    def outputs_dx(h, slot):
        for b in range(n_piece):
            cols = slice(b * gcol, (b + 1) * gcol)
            dxacc_v[:, cols] += mm_nt(do_v[h], wq_v[slot, cols, :])

    x_copy = pltpu.make_async_copy(x_hbm, x_v, in_sem.at[0])
    dy_copy = pltpu.make_async_copy(dy_hbm, dy_v, in_sem.at[1])
    x_copy.start()
    wk_in = small_copies(wk_hbm, p_v, 0)
    wv_in = small_copies(wv_hbm, ds_v, n_chip)
    for copy in wk_in:
        copy.start()

    barrier = pltpu.get_barrier_semaphore()
    for dev in (near[UP], near[DOWN], mate):
        pl.semaphore_signal(barrier, inc=1, device_id={"cp": dev}, device_id_type=MESH)

    yacc_v[...] = jnp.zeros_like(yacc_v)
    dxacc_v[...] = jnp.zeros_like(dxacc_v)
    for copy in wv_in:
        copy.start()
    x_copy.wait()

    def project_small(buf, which):
        acc = [None, None]
        for i in range(n_chip):
            b, half = i // 2, i % 2
            term = mm(x_v[:, b * gcol:(b + 1) * gcol], buf[i])
            acc[half] = term if b == 0 else acc[half] + term
        for h in range(kv_heads):
            col = (h % 2) * hd
            kv_v[h, me, which] = acc[h // 2][:, col:col + hd].astype(BF)

    for copy in wk_in:
        copy.wait()
    slab_q(2, 0).start()
    project_small(p_v, 0)
    for copy in wv_in:
        copy.wait()
    dy_copy.start()
    project_small(ds_v, 1)
    slab_o(2, 0).start()
    pl.semaphore_wait(barrier, 3)
    ag_start(0)
    ag_start(1)

    slab_q(2, 0).wait()
    slab_q(1, 1).start()
    project_q(2, 0)
    slab_o(1, 1).start()
    dy_copy.wait()
    slab_o(2, 0).wait()
    slab_q(0, 0).start()
    project_do(2, 0, 0)
    ag_level(0, 1)
    project_do(2, 0, 1)
    slab_o(0, 0).start()
    ag_level(1, 1)
    slab_q(1, 1).wait()
    project_q(1, 1)
    ag_level(0, 2)
    slab_o(1, 1).wait()
    project_do(1, 1, 0)
    ag_level(1, 2)
    ag_start(2)
    project_do(1, 1, 1)
    ag_level(0, 3)
    slab_q(0, 0).wait()
    project_q(0, 0)
    ag_level(1, 3)
    slab_o(0, 0).wait()
    project_do(0, 0, 0)
    ag_level(0, 4)
    ag_level(2, 1)
    ag_start(3)
    project_do(0, 0, 1)
    ag_level(1, 4)

    first_serve = {-2: [(2, 2)], 1: [(3, 1)], 2: [(2, 3)], 4: [(3, 2)], 5: [(2, 4)], 7: [(3, 3)]}

    def head_step(h, carry):
        def serve(b):
            if b in first_serve:
                @pl.when(h == 0)
                def _():
                    for g, hop in first_serve[b]:
                        ag_level(g, hop)
            if b in (-2, 1, 4, 6):
                @pl.when((h == 1) | (h == 3))
                def _():
                    if b == -2:
                        @pl.when(h == 3)
                        def _():
                            rs_step(h - 2, 0, 3)
                        rs_step(h - 1, 0, 1)
                    elif b == 1:
                        rs_step(h - 1, 1, 1)
                    elif b == 4:
                        rs_step(h - 1, 0, 2)

                        @pl.when(h == 3)
                        def _():
                            rs_end(h - 2)
                    else:
                        rs_step(h - 1, 1, 2)
            if b in (3, 5):
                @pl.when(h == 2)
                def _():
                    if b == 3:
                        rs_end(h - 2)
                        rs_step(h - 1, 0, 1)
                    else:
                        rs_step(h - 1, 1, 1)

        ag_finish(h)
        transpose_kv(h)
        attend(h, serve)
        key_grads(h)

        @pl.when(h == 2)
        def _():
            rs_step(h - 1, 0, 2)

        rs_begin(h)

        @pl.when(h == 0)
        def _():
            outputs_y(h, 0)
            slab_o(3, 0).start()
            ag_level(3, 4)
            outputs_dx(h, 0)
            slab_q(3, 0).start()

        @pl.when(h == 1)
        def _():
            rs_step(h - 1, 0, 3)

        @pl.when(h == 2)
        def _():
            slab_q(3, 0).wait()
            project_q(3, 0)
            rs_step(h - 1, 1, 2)
            slab_o(3, 0).wait()
            project_do(3, 0, 0)
            project_do(3, 0, 1)

        return carry

    lax.fori_loop(0, kv_heads, head_step, 0)

    last = kv_heads - 1
    wk_in = small_copies(wk_hbm, p_v, 0)
    wv_in = small_copies(wv_hbm, ds_v, n_chip)
    for copy in wk_in + wv_in:
        copy.start()

    def fin_wait(h):
        remote(fout_v.at[h], fin_v.at[1 - core, h], fin_send.at[h], fin_recv.at[h], mate).wait_recv()

    def dx_copy(b):
        cols = pl.ds(b * gcol, gcol)
        return pltpu.make_async_copy(dy_v.at[:, cols], dx_hbm.at[:, cols], out_sem.at[b])

    def key_outputs(half, store):
        pair = (2 * half, 2 * half + 1)
        gk = jnp.concatenate([fin_v[0, h].T for h in pair], axis=1)
        gv = jnp.concatenate([fin_v[1, h].T for h in pair], axis=1)
        for b in range(n_piece):
            cols = slice(b * gcol, (b + 1) * gcol)
            i = 2 * b + half
            total = dxacc_v[:, cols] + mm_nt(gk, p_v[i]) + mm_nt(gv, ds_v[i])
            if store:
                dy_v[:, cols] = total.astype(BF)
                dx_copy(b).start()
            else:
                dxacc_v[:, cols] = total

    rs_step(2, 0, 3)
    outputs_y(1, 1)
    slab_o(2, 1).start()
    outputs_dx(1, 1)
    slab_q(2, 1).start()
    rs_step(3, 0, 1)
    outputs_y(3, 0)
    rs_step(3, 1, 1)
    outputs_dx(3, 0)
    rs_end(2)
    rs_step(3, 0, 2)
    slab_o(2, 1).wait()
    outputs_y(2, 1)
    x_v[...] = yacc_v[...].astype(BF)
    y_copy = pltpu.make_async_copy(x_v, y_hbm, in_sem.at[0])
    y_copy.start()
    rs_step(3, 1, 2)
    for copy in wk_in + wv_in:
        copy.wait()
    fin_wait(0)
    fin_wait(1)
    key_outputs(0, False)
    rs_step(3, 0, 3)
    slab_q(2, 1).wait()
    outputs_dx(2, 1)
    for h in range(kv_heads):
        ag_drain(h)
    rs_end(3)
    fin_wait(2)
    fin_wait(3)
    key_outputs(1, True)
    for h in range(kv_heads):
        fin_copy(h).wait_send()
    y_copy.wait()
    for b in range(n_piece):
        dx_copy(b).wait()


def store_kernel(y_in, dx_in, y_out, dx_out, buf, in_sem, out_sem):
    n_part, rows = buf.shape[0] // 2, buf.shape[1]
    pairs = []
    for i in range(2 * n_part):
        src, dst = ((y_in, y_out), (dx_in, dx_out))[i // n_part]
        at = pl.ds((i % n_part) * rows, rows)
        pairs.append((pltpu.make_async_copy(src.at[at], buf.at[i], in_sem.at[i]),
                      pltpu.make_async_copy(buf.at[i], dst.at[at], out_sem.at[i])))
    for take, _ in pairs:
        take.start()
    for take, give in pairs:
        take.wait()
        give.start()
    for _, give in pairs:
        give.wait()


def solution(mesh):
    n_dev = mesh.shape["cp"]
    row_spec = P(("dp", "cp"), None)
    full_spec = P(None, None)

    def local_body(x_loc, dy_loc, w_q, w_k, w_v, w_o):
        tok, width = x_loc.shape
        q_heads = w_q.shape[1] // HEAD_DIM
        kv_heads = w_k.shape[1] // HEAD_DIM
        q_group = q_heads // kv_heads
        gcol = q_group * HEAD_DIM
        n_chip = n_dev // 2
        far = n_chip // 2
        chunk = 2 * tok
        hd = HEAD_DIM
        any_spec = pl.BlockSpec(memory_space=pl.ANY)
        dma = pltpu.SemaphoreType.DMA
        scratch = [
            pltpu.VMEM((tok, width), BF), pltpu.VMEM((tok, width), BF),
            pltpu.VMEM((2, width, gcol), BF), pltpu.VMEM((2, gcol, width), BF),
            pltpu.VMEM((kv_heads, n_dev, 2, tok, hd), BF),
            pltpu.VMEM((n_chip, hd, chunk), BF), pltpu.VMEM((n_chip, hd, chunk), BF),
            pltpu.VMEM((kv_heads, tok, gcol), BF), pltpu.VMEM((kv_heads, tok, gcol), BF),
            pltpu.VMEM((hd, q_group * tok), BF), pltpu.VMEM((hd, q_group * tok), BF),
            pltpu.VMEM((2, n_chip, tok, chunk), F32),
            pltpu.VMEM((n_chip, q_group * tok, chunk), BF), pltpu.VMEM((n_chip, q_group * tok, chunk), BF),
            pltpu.VMEM((2, 2, n_chip, 2, hd, tok), F32), pltpu.VMEM((kv_heads, n_chip, 2, hd, tok), F32),
            pltpu.VMEM((kv_heads, 2, 2 * far - 1, hd, tok), F32),
            pltpu.VMEM((tok, width), F32), pltpu.VMEM((tok, width), F32),
            pltpu.VMEM((2, kv_heads, hd, tok), BF), pltpu.VMEM((kv_heads, hd, tok), BF),
            dma((2,)), dma((2 * n_chip,)), dma((2, 2)),
            dma((kv_heads,)), dma((kv_heads, 4 * far + 1)),
            dma((kv_heads,)), dma((kv_heads, n_chip)),
            dma((kv_heads,)), dma((kv_heads, 2, 2 * far - 1)),
            dma((kv_heads,)), dma((kv_heads,)), dma((width // gcol,)),
        ]
        out = jax.ShapeDtypeStruct((tok, width), BF)
        y, dx = pl.pallas_call(
            functools.partial(layer_kernel, n_dev, kv_heads, q_group),
            out_shape=(out, out),
            in_specs=[any_spec] * 6,
            out_specs=(any_spec, any_spec),
            scratch_shapes=scratch,
            name="layer",
            compiler_params=pltpu.CompilerParams(collective_id=0, has_side_effects=True,
                                                 vmem_limit_bytes=67043328),
        )(x_loc, dy_loc, w_q, w_k, w_v, w_o)
        n_part = 2
        return pl.pallas_call(
            store_kernel,
            out_shape=(out, out),
            in_specs=[any_spec] * 2,
            out_specs=(any_spec, any_spec),
            scratch_shapes=[pltpu.VMEM((2 * n_part, tok // n_part, width), BF),
                            dma((2 * n_part,)), dma((2 * n_part,))],
            name="store",
        )(y, dx)

    return jax.shard_map(local_body, mesh=mesh,
                         in_specs=(row_spec, row_spec, full_spec, full_spec, full_spec, full_spec),
                         out_specs=(row_spec, row_spec), check_vma=False)
```

time: 130 us -> 107 us (0.82)
  Pallas kernels: 125 us -> 106 us
  local copies, waits for them, and re-layouts: 4.32 us -> 0 us
    pallas_call x1, Pallas kernels: 125 us -> 104 us  [local_body(): pl.pallas_call(functools.partial(layer_kernel, n_dev, kv_heads, q_group),...]
    unnamed x2 -> x0, local copies, waits for them, and re-layouts: 4.32 us -> none
    pallas_call x0 -> x1, Pallas kernels: none -> 2.31 us  [local_body(): pl.pallas_call(store_kernel, out_shape=(out, out), in_specs=[any_spec] *...]
where the time goes in v2:
time: 107 us
  Pallas kernels  106 us (99%)
    pallas_call x1, Pallas kernels, local_body(): pl.pallas_call(functools.partial(layer_kernel, n_dev, kv_heads, q_group),...  104 us
    pallas_call x1, Pallas kernels, local_body(): pl.pallas_call(store_kernel, out_shape=(out, out), in_specs=[any_spec] *...  2.31 us

profile of v2, /device:TPU:21, one launch (start us, length us, event | category | flops | bytes accessed | tf_op | source)
XLA Modules:
  0.0 106.8 jit_solution(1450733519003985988)
XLA Ops:
  0.6 103.7 %layer.1 = (bf16[128,3584]{1,0:T(8,128)(2,1)}, bf16[128,3584]{1,0:T(8,128)(2,1)}) custom-call(bf16[128,3584]{1,0:T(8,128)(2,1)} %x_hbm.1, bf16[128,3584]{1,0:T(8,128)(2,1)} %dy_hbm.1, bf16[3584,3584]{1,0:T(8,128)(2,1)} %wq_hbm.1, bf16[3584,512]{1,0:T(8,128)(2,1)} %wk_hbm.1, bf16[3584,512]{1,0:T(8,128)(2,1)} %wv_hbm.1, bf16[3584,3584]{1,0:T(8,128)(2,1)} %wo_hbm.1), custom_call_target="tpu_custom_call" | custom-call | tf_op jit(solution)/shard_map/layer/pallas_call | solution.py:580
  104.3 2.3 %store.1 = (bf16[128,3584]{1,0:T(8,128)(2,1)}, bf16[128,3584]{1,0:T(8,128)(2,1)}) custom-call(bf16[128,3584]{1,0:T(8,128)(2,1)} %get-tuple-element.4.y_in, bf16[128,3584]{1,0:T(8,128)(2,1)} %get-tuple-element.5.dx_in), custom_call_target="tpu_custom_call" | custom-call | tf_op jit(solution)/shard_map/store/pallas_call | solution.py:591

commit v3 on v2

--- a/solution.py
+++ b/solution.py
@@ -51,6 +51,7 @@
         return lax.rem(chip + off + n_chip, n_chip)
 
     near = (2 * chip_at(1) + core, 2 * chip_at(-1) + core)
+    next_near = (2 * chip_at(2) + core, 2 * chip_at(-2) + core)
 
     def remote(src, dst, ssem, rsem, dev):
         return pltpu.make_async_remote_copy(src_ref=src, dst_ref=dst, send_sem=ssem, recv_sem=rsem,
@@ -81,10 +82,10 @@
         ref = ag_view(h, 2 * src_chip(d, hop) + core, d, hop)
         return remote(ref, ref, ag_send.at[h], ag_recv.at[h, d * far + hop - 1], near[d])
 
-    def ag_ring_out(h, d, hop):
-        dev = me if hop == 1 else 2 * src_chip(d, hop - 1) + core
+    def ag_ring_out(h, d, hop, step=1):
+        dev = me if hop == step else 2 * src_chip(d, hop - step) + core
         ref = ag_view(h, dev, d, hop)
-        return remote(ref, ref, ag_send.at[h], ag_recv.at[h, d * far + hop - 1], near[d])
+        return remote(ref, ref, ag_send.at[h], ag_recv.at[h, d * far + hop - 1], (near if step == 1 else next_near)[d])
 
     def ag_mate_own(h):
         ref = kv_v.at[h, me]
@@ -100,15 +101,20 @@
         idx = 2 * far + 1 + d * far + hop - 1
         return remote(ref, ref, ag_send.at[h], ag_recv.at[h, idx], mate)
 
-    def ag_start(h):
+    def ag_start(h, two=False):
         for d in (UP, DOWN):
+            if two:
+                ag_ring_out(h, d, 2, 2).start()
             ag_ring_out(h, d, 1).start()
         ag_mate_own(h).start()
 
-    def ag_level(h, hop):
+    def ag_level(h, hop, two=False):
         for d in (UP, DOWN):
             ag_ring(h, d, hop).wait_recv()
-            if hop < far:
+            if two and hop == 2:
+                ag_ring_out(h, d, 3).start()
+                ag_ring_out(h, d, 4, 2).start()
+            elif hop < far and not two:
                 ag_ring_out(h, d, hop + 1).start()
             ag_mate_out(h, d, hop).start()
 
@@ -204,8 +210,8 @@
 
     do_cut = (gcol // 2 + chunk - 1) // chunk * chunk
 
-    def project_do(h, slot, part):
-        cols = slice(0, do_cut) if part == 0 else slice(do_cut, gcol)
+    def project_do(h, slot, part=None):
+        cols = {None: slice(0, gcol), 0: slice(0, do_cut), 1: slice(do_cut, gcol)}[part]
         do_v[h, :, cols] = mm_nt(dy_v[...], wo_v[slot, cols, :]).astype(BF)
 
     def transpose_kv(h):
@@ -322,7 +328,7 @@
         copy.start()
 
     barrier = pltpu.get_barrier_semaphore()
-    for dev in (near[UP], near[DOWN], mate):
+    for dev in near + next_near + (mate,):
         pl.semaphore_signal(barrier, inc=1, device_id={"cp": dev}, device_id_type=MESH)
 
     yacc_v[...] = jnp.zeros_like(yacc_v)
@@ -350,9 +356,8 @@
     dy_copy.start()
     project_small(ds_v, 1)
     slab_o(2, 0).start()
-    pl.semaphore_wait(barrier, 3)
-    ag_start(0)
-    ag_start(1)
+    pl.semaphore_wait(barrier, 5)
+    ag_start(0, True)
 
     slab_q(2, 0).wait()
     slab_q(1, 1).start()
@@ -361,32 +366,23 @@
     dy_copy.wait()
     slab_o(2, 0).wait()
     slab_q(0, 0).start()
-    project_do(2, 0, 0)
-    ag_level(0, 1)
-    project_do(2, 0, 1)
+    project_do(2, 0)
     slab_o(0, 0).start()
-    ag_level(1, 1)
     slab_q(1, 1).wait()
     project_q(1, 1)
-    ag_level(0, 2)
+    ag_level(0, 2, True)
+    ag_level(0, 1, True)
+    ag_start(1, True)
     slab_o(1, 1).wait()
-    project_do(1, 1, 0)
-    ag_level(1, 2)
-    ag_start(2)
-    project_do(1, 1, 1)
-    ag_level(0, 3)
+    project_do(1, 1)
     slab_q(0, 0).wait()
     project_q(0, 0)
-    ag_level(1, 3)
+    ag_level(0, 3, True)
     slab_o(0, 0).wait()
-    project_do(0, 0, 0)
-    ag_level(0, 4)
-    ag_level(2, 1)
-    ag_start(3)
-    project_do(0, 0, 1)
-    ag_level(1, 4)
-
-    first_serve = {-2: [(2, 2)], 1: [(3, 1)], 2: [(2, 3)], 4: [(3, 2)], 5: [(2, 4)], 7: [(3, 3)]}
+    project_do(0, 0)
+    ag_level(0, 4, True)
+
+    first_serve = {-2: [(1, 2)], 1: [(1, 1)], 4: [(1, 3)], 6: [(1, 4)], 7: [(2, 1)]}
 
     def head_step(h, carry):
         def serve(b):
@@ -394,65 +390,77 @@
                 @pl.when(h == 0)
                 def _():
                     for g, hop in first_serve[b]:
-                        ag_level(g, hop)
-            if b in (-2, 1, 4, 6):
-                @pl.when((h == 1) | (h == 3))
+                        ag_level(g, hop, g < 2)
+                    if b in (1, 4):
+                        ag_start(2 if b == 1 else 3)
+            if b in (-1, 2, 5, 7):
+                @pl.when(h == 1)
                 def _():
-                    if b == -2:
-                        @pl.when(h == 3)
-                        def _():
-                            rs_step(h - 2, 0, 3)
+                    if b == -1:
                         rs_step(h - 1, 0, 1)
-                    elif b == 1:
+                    elif b == 2:
                         rs_step(h - 1, 1, 1)
-                    elif b == 4:
+                        ag_level(2, 3)
+                    elif b == 5:
                         rs_step(h - 1, 0, 2)
-
-                        @pl.when(h == 3)
-                        def _():
-                            rs_end(h - 2)
+                        ag_level(3, 3)
                     else:
                         rs_step(h - 1, 1, 2)
-            if b in (3, 5):
+            if b in (1, 5, 6, 7):
                 @pl.when(h == 2)
                 def _():
-                    if b == 3:
+                    if b == 1:
+                        ag_level(3, 4)
+                    elif b == 5:
+                        rs_step(h - 1, 0, 1)
+                    elif b == 6:
+                        rs_step(h - 1, 1, 1)
+                    else:
                         rs_end(h - 2)
+            if b in (0, 1, 3, 6, 7):
+                @pl.when(h == 3)
+                def _():
+                    if b == 0:
+                        rs_step(h - 2, 0, 3)
+                    elif b == 1:
                         rs_step(h - 1, 0, 1)
+                    elif b == 3:
+                        rs_step(h - 1, 1, 1)
+                    elif b == 6:
+                        rs_step(h - 1, 0, 2)
                     else:
-                        rs_step(h - 1, 1, 1)
+                        rs_end(h - 2)
 
         ag_finish(h)
         transpose_kv(h)
         attend(h, serve)
         key_grads(h)
 
-        @pl.when(h == 2)
+        @pl.when(h == 1)
         def _():
-            rs_step(h - 1, 0, 2)
+            ag_level(2, 4)
+            rs_step(h - 1, 0, 3)
 
         rs_begin(h)
 
         @pl.when(h == 0)
         def _():
+            ag_level(3, 1)
             outputs_y(h, 0)
             slab_o(3, 0).start()
-            ag_level(3, 4)
+            ag_level(2, 2)
             outputs_dx(h, 0)
             slab_q(3, 0).start()
-
-        @pl.when(h == 1)
-        def _():
-            rs_step(h - 1, 0, 3)
+            ag_level(3, 2)
 
         @pl.when(h == 2)
         def _():
             slab_q(3, 0).wait()
             project_q(3, 0)
+            rs_step(h - 1, 0, 2)
             rs_step(h - 1, 1, 2)
             slab_o(3, 0).wait()
-            project_do(3, 0, 0)
-            project_do(3, 0, 1)
+            project_do(3, 0)
 
         return carry
 
@@ -485,8 +493,9 @@
             else:
                 dxacc_v[:, cols] = total
 
+    rs_step(2, 1, 2)
+    outputs_y(1, 1)
     rs_step(2, 0, 3)
-    outputs_y(1, 1)
     slab_o(2, 1).start()
     outputs_dx(1, 1)
     slab_q(2, 1).start()

time: 107 us -> 103 us (0.963)
  Pallas kernels: 106 us -> 102 us
    pallas_call x1, Pallas kernels: 104 us -> 100 us  [local_body(): pl.pallas_call(functools.partial(layer_kernel, n_dev, kv_heads, q_group),...]
where the time goes in v3:
time: 103 us
  Pallas kernels  102 us (99%)
    pallas_call x1, Pallas kernels, local_body(): pl.pallas_call(functools.partial(layer_kernel, n_dev, kv_heads, q_group),...  100 us
    pallas_call x1, Pallas kernels, local_body(): pl.pallas_call(store_kernel, out_shape=(out, out), in_specs=[any_spec] *...  2.31 us

profile of v3, /device:TPU:21, one launch (start us, length us, event | category | flops | bytes accessed | tf_op | source)
XLA Modules:
  0.0 103.3 jit_solution(2624772513930383062)
XLA Ops:
  0.6 100.1 %layer.1 = (bf16[128,3584]{1,0:T(8,128)(2,1)}, bf16[128,3584]{1,0:T(8,128)(2,1)}) custom-call(bf16[128,3584]{1,0:T(8,128)(2,1)} %x_hbm.1, bf16[128,3584]{1,0:T(8,128)(2,1)} %dy_hbm.1, bf16[3584,3584]{1,0:T(8,128)(2,1)} %wq_hbm.1, bf16[3584,512]{1,0:T(8,128)(2,1)} %wk_hbm.1, bf16[3584,512]{1,0:T(8,128)(2,1)} %wv_hbm.1, bf16[3584,3584]{1,0:T(8,128)(2,1)} %wo_hbm.1), custom_call_target="tpu_custom_call" | custom-call | tf_op jit(solution)/shard_map/layer/pallas_call | solution.py:589
  100.8 2.3 %store.1 = (bf16[128,3584]{1,0:T(8,128)(2,1)}, bf16[128,3584]{1,0:T(8,128)(2,1)}) custom-call(bf16[128,3584]{1,0:T(8,128)(2,1)} %get-tuple-element.4.y_in, bf16[128,3584]{1,0:T(8,128)(2,1)} %get-tuple-element.5.dx_in), custom_call_target="tpu_custom_call" | custom-call | tf_op jit(solution)/shard_map/store/pallas_call | solution.py:600

commit v4 on v3

--- a/solution.py
+++ b/solution.py
@@ -393,42 +393,43 @@
                         ag_level(g, hop, g < 2)
                     if b in (1, 4):
                         ag_start(2 if b == 1 else 3)
-            if b in (-1, 2, 5, 7):
+            if b in (-1, 2, 4, 5, 7):
                 @pl.when(h == 1)
                 def _():
                     if b == -1:
                         rs_step(h - 1, 0, 1)
                     elif b == 2:
                         rs_step(h - 1, 1, 1)
+                    elif b == 4:
                         ag_level(2, 3)
                     elif b == 5:
                         rs_step(h - 1, 0, 2)
-                        ag_level(3, 3)
                     else:
                         rs_step(h - 1, 1, 2)
+                        ag_level(2, 4)
+                        ag_level(3, 2)
             if b in (1, 5, 6, 7):
                 @pl.when(h == 2)
                 def _():
                     if b == 1:
-                        ag_level(3, 4)
+                        ag_level(3, 3)
                     elif b == 5:
                         rs_step(h - 1, 0, 1)
                     elif b == 6:
                         rs_step(h - 1, 1, 1)
                     else:
                         rs_end(h - 2)
-            if b in (0, 1, 3, 6, 7):
+                        ag_level(3, 4)
+            if b in (1, 3, 7):
                 @pl.when(h == 3)
                 def _():
-                    if b == 0:
+                    if b == 1:
                         rs_step(h - 2, 0, 3)
-                    elif b == 1:
                         rs_step(h - 1, 0, 1)
                     elif b == 3:
                         rs_step(h - 1, 1, 1)
-                    elif b == 6:
+                    else:
                         rs_step(h - 1, 0, 2)
-                    else:
                         rs_end(h - 2)
 
         ag_finish(h)
@@ -438,26 +439,30 @@
 
         @pl.when(h == 1)
         def _():
-            ag_level(2, 4)
             rs_step(h - 1, 0, 3)
-
-        rs_begin(h)
-
-        @pl.when(h == 0)
-        def _():
-            ag_level(3, 1)
-            outputs_y(h, 0)
-            slab_o(3, 0).start()
-            ag_level(2, 2)
-            outputs_dx(h, 0)
-            slab_q(3, 0).start()
-            ag_level(3, 2)
 
         @pl.when(h == 2)
         def _():
             slab_q(3, 0).wait()
             project_q(3, 0)
             rs_step(h - 1, 0, 2)
+
+        @pl.when(h == 0)
+        def _():
+            outputs_y(h, 0)
+            slab_o(3, 0).start()
+
+        rs_begin(h)
+
+        @pl.when(h == 0)
+        def _():
+            ag_level(3, 1)
+            ag_level(2, 2)
+            outputs_dx(h, 0)
+            slab_q(3, 0).start()
+
+        @pl.when(h == 2)
+        def _():
             rs_step(h - 1, 1, 2)
             slab_o(3, 0).wait()
             project_do(3, 0)

time: 103 us -> 99.9 us (0.970)
  Pallas kernels: 102 us -> 98.9 us
    pallas_call x1, Pallas kernels: 100 us -> 96.6 us  [local_body(): pl.pallas_call(functools.partial(layer_kernel, n_dev, kv_heads, q_group),...]
where the time goes in v4:
time: 99.9 us; the launch traced here: 99.8 us
  Pallas kernels  98.9 us (99%)
    pallas_call x1, Pallas kernels, local_body(): pl.pallas_call(functools.partial(layer_kernel, n_dev, kv_heads, q_group),...  96.6 us
    pallas_call x1, Pallas kernels, local_body(): pl.pallas_call(store_kernel, out_shape=(out, out), in_specs=[any_spec] *...  2.31 us

profile of v4, /device:TPU:21, one launch (start us, length us, event | category | flops | bytes accessed | tf_op | source)
XLA Modules:
  0.0 99.8 jit_solution(14550712682987728495)
XLA Ops:
  0.6 96.6 %layer.1 = (bf16[128,3584]{1,0:T(8,128)(2,1)}, bf16[128,3584]{1,0:T(8,128)(2,1)}) custom-call(bf16[128,3584]{1,0:T(8,128)(2,1)} %x_hbm.1, bf16[128,3584]{1,0:T(8,128)(2,1)} %dy_hbm.1, bf16[3584,3584]{1,0:T(8,128)(2,1)} %wq_hbm.1, bf16[3584,512]{1,0:T(8,128)(2,1)} %wk_hbm.1, bf16[3584,512]{1,0:T(8,128)(2,1)} %wv_hbm.1, bf16[3584,3584]{1,0:T(8,128)(2,1)} %wo_hbm.1), custom_call_target="tpu_custom_call" | custom-call | tf_op jit(solution)/shard_map/layer/pallas_call | solution.py:594
  97.3 2.3 %store.1 = (bf16[128,3584]{1,0:T(8,128)(2,1)}, bf16[128,3584]{1,0:T(8,128)(2,1)}) custom-call(bf16[128,3584]{1,0:T(8,128)(2,1)} %get-tuple-element.4.y_in, bf16[128,3584]{1,0:T(8,128)(2,1)} %get-tuple-element.5.dx_in), custom_call_target="tpu_custom_call" | custom-call | tf_op jit(solution)/shard_map/store/pallas_call | solution.py:605

commit v5 on v4

--- a/solution.py
+++ b/solution.py
@@ -406,7 +406,6 @@
                         rs_step(h - 1, 0, 2)
                     else:
                         rs_step(h - 1, 1, 2)
-                        ag_level(2, 4)
                         ag_level(3, 2)
             if b in (1, 5, 6, 7):
                 @pl.when(h == 2)
@@ -439,30 +438,28 @@
 
         @pl.when(h == 1)
         def _():
+            ag_level(2, 4)
             rs_step(h - 1, 0, 3)
+
+        @pl.when(h == 2)
+        def _():
+            rs_step(h - 1, 0, 2)
+
+        rs_begin(h)
+
+        @pl.when(h == 0)
+        def _():
+            ag_level(3, 1)
+            outputs_y(h, 0)
+            slab_o(3, 0).start()
+            ag_level(2, 2)
+            outputs_dx(h, 0)
+            slab_q(3, 0).start()
 
         @pl.when(h == 2)
         def _():
             slab_q(3, 0).wait()
             project_q(3, 0)
-            rs_step(h - 1, 0, 2)
-
-        @pl.when(h == 0)
-        def _():
-            outputs_y(h, 0)
-            slab_o(3, 0).start()
-
-        rs_begin(h)
-
-        @pl.when(h == 0)
-        def _():
-            ag_level(3, 1)
-            ag_level(2, 2)
-            outputs_dx(h, 0)
-            slab_q(3, 0).start()
-
-        @pl.when(h == 2)
-        def _():
             rs_step(h - 1, 1, 2)
             slab_o(3, 0).wait()
             project_do(3, 0)

time: 99.9 us -> 98.7 us (0.988)
  Pallas kernels: 98.9 us -> 97.8 us
    pallas_call x1, Pallas kernels: 96.6 us -> 95.5 us  [local_body(): pl.pallas_call(functools.partial(layer_kernel, n_dev, kv_heads, q_group),...]
where the time goes in v5:
time: 98.7 us; the launch traced here: 98.6 us
  Pallas kernels  97.8 us (99%)
    pallas_call x1, Pallas kernels, local_body(): pl.pallas_call(functools.partial(layer_kernel, n_dev, kv_heads, q_group),...  95.5 us
    pallas_call x1, Pallas kernels, local_body(): pl.pallas_call(store_kernel, out_shape=(out, out), in_specs=[any_spec] *...  2.31 us

profile of v5, /device:TPU:21, one launch (start us, length us, event | category | flops | bytes accessed | tf_op | source)
XLA Modules:
  0.0 98.6 jit_solution(7979256116025235709)
XLA Ops:
  0.6 95.5 %layer.1 = (bf16[128,3584]{1,0:T(8,128)(2,1)}, bf16[128,3584]{1,0:T(8,128)(2,1)}) custom-call(bf16[128,3584]{1,0:T(8,128)(2,1)} %x_hbm.1, bf16[128,3584]{1,0:T(8,128)(2,1)} %dy_hbm.1, bf16[3584,3584]{1,0:T(8,128)(2,1)} %wq_hbm.1, bf16[3584,512]{1,0:T(8,128)(2,1)} %wk_hbm.1, bf16[3584,512]{1,0:T(8,128)(2,1)} %wv_hbm.1, bf16[3584,3584]{1,0:T(8,128)(2,1)} %wo_hbm.1), custom_call_target="tpu_custom_call" | custom-call | tf_op jit(solution)/shard_map/layer/pallas_call | solution.py:591
  96.1 2.3 %store.1 = (bf16[128,3584]{1,0:T(8,128)(2,1)}, bf16[128,3584]{1,0:T(8,128)(2,1)}) custom-call(bf16[128,3584]{1,0:T(8,128)(2,1)} %get-tuple-element.4.y_in, bf16[128,3584]{1,0:T(8,128)(2,1)} %get-tuple-element.5.dx_in), custom_call_target="tpu_custom_call" | custom-call | tf_op jit(solution)/shard_map/store/pallas_call | solution.py:602
